TPU v7x, 32 devices: a whole 2x2x4 slice. The times are simulated.
32 devices in a mesh: grp: 8 (over z, core), tp: 4 (over y, x).
Axes of the slice: x: 2, y: 2, z: 4, core: 2. Of those that a mesh axis runs over, the one named last changes fastest.
Arguments:
- tokens: bfloat16 [8192, 8192], P('grp'), may hold values from -12 to 12
- joined_weight: bfloat16 [8192, 10240], P(('grp', 'tp')), may hold values from -1.14904852 to 1.14904852
- rollout_lengths: int32 [64], P('grp'), may hold values from 1 to 128
- prompt_of: int32 [64, 1], P('grp'), may hold values from 0 to 7
- score_weight: bfloat16 [8192], P('tp'), may hold values from -0.52734375 to 0.52734375
Outputs:
- attention: bfloat16 [8192, 8192], P('grp', 'tp')
- advantages: float32 [64], P('grp')
All inputs are finite; a program needn't handle non-finite values.
Results may differ from a plain program's by a relative error of at most 0.012.
The roundings to bfloat16 on the way count: a program that leaves them out, or rounds other values in their place, can miss the bound.
Values may be sent and summed in bfloat16 or wider, within the bound.
A program may use at most 128 MiB of HBM per device.

v0:
```python
import functools

import jax
import jax.numpy as jnp
from jax import lax
from jax.experimental import pallas as pl
from jax.experimental.pallas import tpu as pltpu
from jax.sharding import PartitionSpec as P

QUERY_HEADS = 64
KV_HEAD_COUNT = 8
HEAD_SIZE = 128
CORES = 2
CHUNKS = 5


def attend_kernel(groups, chunks, lengths_ref, flag_ref, weight_ref, own, extra, out_ref, reward_ref):
    ratio = QUERY_HEADS // KV_HEAD_COUNT
    per_chunk = own.shape[2] // HEAD_SIZE
    slot = own.shape[1]
    length = lengths_ref[pl.program_id(0)]
    at_end = flag_ref[0] > 0

    def head(index):
        c, h = divmod(index, per_chunk)
        cols = slice(h * HEAD_SIZE, (h + 1) * HEAD_SIZE)
        added = jnp.where(at_end, extra[c, :, cols].astype(jnp.float32), jnp.float32(0.0))
        return (own[c, :, cols] + added).astype(jnp.bfloat16)

    s_pos = lax.broadcasted_iota(jnp.int32, (slot, slot), 0)
    t_pos = lax.broadcasted_iota(jnp.int32, (slot, slot), 1)
    allowed = ((t_pos <= s_pos) & (t_pos < length))[None]
    live = lax.broadcasted_iota(jnp.int32, (slot, HEAD_SIZE), 0) < length
    total = jnp.zeros((slot, HEAD_SIZE), jnp.float32)
    for g in range(groups):
        base = g * (ratio + 2)
        key = head(base + ratio)
        value = head(base + ratio + 1)
        queries = jnp.concatenate([head(base + a) for a in range(ratio)], axis=0)
        scores = lax.dot_general(
            queries, key, (((1,), (1,)), ((), ())), preferred_element_type=jnp.float32
        ) * HEAD_SIZE ** (-0.5)
        scores = jnp.where(allowed, scores.reshape(ratio, slot, slot), jnp.float32(-1e30))
        expo = jnp.exp(scores - jnp.max(scores, axis=-1, keepdims=True))
        probs = expo * (1.0 / jnp.sum(expo, axis=-1, keepdims=True))
        probs = probs.astype(jnp.bfloat16).reshape(ratio * slot, slot)
        mixed = jnp.dot(probs, value, preferred_element_type=jnp.float32).astype(jnp.bfloat16)
        for a in range(ratio):
            part = mixed[a * slot : (a + 1) * slot]
            cols = slice((g * ratio + a) * HEAD_SIZE, (g * ratio + a + 1) * HEAD_SIZE)
            out_ref[:, cols] = part
            total += part.astype(jnp.float32) * weight_ref[:, cols].astype(jnp.float32)
    summed = jnp.sum(jnp.where(live, total, jnp.float32(0.0)), axis=0, keepdims=True)
    summed = jnp.sum(summed, axis=1, keepdims=True)
    reward_ref[...] = jnp.broadcast_to(summed[None], reward_ref.shape)


def attend(own, extra, lengths, flag, score_weight):
    chunks, rows, width = own.shape
    rollouts = lengths.shape[0]
    slot = rows // rollouts
    features = score_weight.shape[0]
    ratio = QUERY_HEADS // KV_HEAD_COUNT
    block = pl.BlockSpec((chunks, slot, width), lambda r, *_: (0, r, 0))
    attention, reward = pl.pallas_call(
        functools.partial(attend_kernel, features // (ratio * HEAD_SIZE), chunks),
        grid_spec=pltpu.PrefetchScalarGridSpec(
            num_scalar_prefetch=2,
            grid=(rollouts,),
            in_specs=[pl.BlockSpec((1, features), lambda r, *_: (0, 0)), block, block],
            out_specs=[
                pl.BlockSpec((slot, features), lambda r, *_: (r, 0)),
                pl.BlockSpec((1, 8, HEAD_SIZE), lambda r, *_: (r, 0, 0)),
            ],
        ),
        out_shape=[
            jax.ShapeDtypeStruct((rows, features), jnp.bfloat16),
            jax.ShapeDtypeStruct((rollouts, 8, HEAD_SIZE), jnp.float32),
        ],
    )(lengths, flag, score_weight.reshape(1, features), own, extra)
    return attention, reward[:, 0, 0]


def project_kernel(
    n, tp_count, tokens, weight, own_out, extra, gath, far, prod,
    tok_v, far_v, w_v, acc, pbuf, send, recv, loads, w_sem, misc,
):
    g = lax.axis_index("grp")
    t = lax.axis_index("tp")
    z, core = g // CORES, g % CORES
    rows, depth = tokens.shape
    chunks, _, width = gath.shape
    own_rows = weight.shape[0]
    half = own_rows * tp_count
    plane = half * CORES
    columns = width * chunks
    part = rows // tp_count
    far_cols = far.shape[1]
    steps = n - 2
    inner = (z >= 1) & (z <= n - 2)
    helper = (z == 1) | (z == n - 2)
    at_end = (z == 0) | (z == n - 1)
    first_far = jnp.where(z < n // 2, 2, 0)
    ids = {}

    def sem(key):
        return ids.setdefault(key, len(ids))

    def remote(key, src, dst, device):
        i = sem(key)
        return pltpu.make_async_remote_copy(
            src_ref=src, dst_ref=dst, send_sem=send.at[i], recv_sem=recv.at[i],
            device_id=device, device_id_type=pl.DeviceIdType.MESH,
        )

    sends = []

    def start(cond, key, src, dst, device):
        @pl.when(cond)
        def _():
            remote(key, src, dst, device).start()

        sends.append((cond, key, src, dst, device))

    def arrived(cond, key, dst):
        @pl.when(cond)
        def _():
            remote(key, dst, dst, (g, t)).wait_recv()

    always = z >= 0
    sibling = (g + 1 - 2 * core, t)

    def piece(q, who):
        return gath.at[q, pl.ds(pl.multiple_of(z * plane + core * half + who * own_rows, own_rows), own_rows)]

    def block(q, p, c):
        return gath.at[q, pl.ds(pl.multiple_of(p * plane + c * half, half), half)]

    def columns_of(who, q):
        return weight.at[:, pl.ds(pl.multiple_of(who * columns + q * width, width), width)]

    def scatter(q):
        pltpu.make_async_copy(columns_of(t, q), piece(q, t), loads.at[q]).start()
        for d in range(1, tp_count):
            start(always, ("a", q, d), columns_of(t ^ d, q), piece(q, t), (g, t ^ d))

    def gathered(q):
        pltpu.make_async_copy(columns_of(t, q), piece(q, t), loads.at[q]).wait()
        for d in range(1, tp_count):
            arrived(always, ("a", q, d), piece(q, t ^ d))

    def launch(q):
        mine = block(q, z, core)
        start(z >= 1, ("l", q, 1), mine, mine, (g - CORES, t))
        start(z <= n - 2, ("r", q, 1), mine, mine, (g + CORES, t))
        start(always, ("s", q), mine, mine, sibling)

    def has(side, s):
        reach = (z + s <= n - 1) if side == "l" else (z - s >= 0)
        return reach if s == 1 else reach & inner

    def forward(q, s):
        for side, sign in (("l", 1), ("r", -1)):
            here = jnp.clip(z + sign * s, 0, n - 1)
            got = block(q, here, core)
            arrived(has(side, s), (side, q, s), got)
            if s < steps:
                more = (z >= 2) if side == "l" else (z <= n - 3)
                start(has(side, s) & more, (side, q, s + 1), got, got, (g - sign * CORES, t))
            start(has(side, s), ("s" + side, q, s), got, got, sibling)

    def swapped(q):
        arrived(always, ("s", q), block(q, z, 1 - core))
        for s in range(1, steps + 1):
            for side, sign in (("l", 1), ("r", -1)):
                here = jnp.clip(z + sign * s, 0, n - 1)
                arrived(has(side, s), ("s" + side, q, s), block(q, here, 1 - core))

    tile = 256

    def gemm(q, lhs, low, high, origin):
        def load(p):
            return pltpu.make_async_copy(
                gath.at[q, pl.ds(pl.multiple_of(p * plane, plane), plane)], w_v.at[p % 2], w_sem.at[p % 2]
            )

        load(low).start()
        acc[...] = jnp.zeros_like(acc)

        def step(p, carry):
            @pl.when(p + 1 < high)
            def _():
                load(p + 1).start()

            load(p).wait()
            cols = pl.ds(pl.multiple_of((p - origin) * plane, plane), plane)

            def rows_step(m, carry):
                at = pl.ds(pl.multiple_of(m * tile, tile), tile)
                acc[at, :] += jnp.dot(lhs[at, cols], w_v[p % 2], preferred_element_type=jnp.float32)
                return carry

            return lax.fori_loop(0, rows // tile, rows_step, carry)

        lax.fori_loop(low, high, step, 0)

    def compute(q):
        low = jnp.where(z == n - 1, n - 2, 0)
        high = jnp.where(z == 0, 2, n)
        gemm(q, tok_v, low, high, 0)
        out = pltpu.make_async_copy(acc, own_out.at[q], misc.at[1])
        out.start()
        out.wait()

    def assist(q):
        @pl.when(helper)
        def _():
            gemm(q, far_v, first_far, first_far + steps, first_far)
            pbuf[...] = acc[...].astype(pbuf.dtype)
            out = pltpu.make_async_copy(pbuf, prod.at[q], misc.at[2])
            out.start()
            out.wait()

        start(helper, ("p", q), prod.at[q], extra.at[q], (jnp.where(z == 1, g - CORES, g + CORES), t))

    def token_rows(who):
        return far.at[pl.ds(pl.multiple_of(who * part, part), part)]

    load_tokens = pltpu.make_async_copy(tokens, tok_v, misc.at[0])
    far_source = tokens.at[
        pl.ds(pl.multiple_of(t * part, part), part),
        pl.ds(pl.multiple_of(first_far * plane, plane), far_cols),
    ]
    start(at_end, ("t",), far_source, token_rows(t), (jnp.where(z == 0, g + CORES, g - CORES), t))
    for q in range(chunks):
        scatter(q)
    load_tokens.start()
    for q in range(chunks):
        gathered(q)
        launch(q)
    arrived(helper, ("t",), token_rows(t))
    for d in range(1, tp_count):
        start(helper, ("g", d), token_rows(t), token_rows(t), (g, t ^ d))
    load_tokens.wait()
    for q in range(chunks - 1):
        forward(q, 1)
    for q in range(chunks):
        for s in range(2, steps + 1):
            forward(q, s)
        swapped(q)
        if q == 0:
            for d in range(1, tp_count):
                arrived(helper, ("g", d), token_rows(t ^ d))

            @pl.when(helper)
            def _():
                fill = pltpu.make_async_copy(far, far_v, misc.at[0])
                fill.start()
                fill.wait()

        assist(q)
        if q == 0:
            forward(chunks - 1, 1)
        compute(q)
    for q in range(chunks):
        arrived(at_end, ("p", q), extra.at[q])
    for cond, key, src, dst, device in sends:
        @pl.when(cond)
        def _():
            remote(key, src, dst, device).wait_send()


def project(tokens, weight, n, tp_count):
    rows, depth = tokens.shape
    own_rows = weight.shape[0]
    width = weight.shape[1] // tp_count // CHUNKS
    plane = own_rows * tp_count * CORES
    far = plane * (n - 2)
    flows = CHUNKS * (tp_count + 1 + 4 * (n - 2)) + tp_count
    anywhere = pl.BlockSpec(memory_space=pl.ANY)
    own, extra, *_ = pl.pallas_call(
        functools.partial(project_kernel, n, tp_count),
        in_specs=[anywhere] * 2,
        out_specs=[anywhere] * 5,
        out_shape=[
            jax.ShapeDtypeStruct((CHUNKS, rows, width), jnp.float32),
            jax.ShapeDtypeStruct((CHUNKS, rows, width), jnp.bfloat16),
            jax.ShapeDtypeStruct((CHUNKS, depth, width), jnp.bfloat16),
            jax.ShapeDtypeStruct((rows, far), jnp.bfloat16),
            jax.ShapeDtypeStruct((CHUNKS, rows, width), jnp.bfloat16),
        ],
        scratch_shapes=[
            pltpu.VMEM((rows, depth), jnp.bfloat16),
            pltpu.VMEM((rows, far), jnp.bfloat16),
            pltpu.VMEM((2, plane, width), jnp.bfloat16),
            pltpu.VMEM((rows, width), jnp.float32),
            pltpu.VMEM((rows, width), jnp.bfloat16),
            pltpu.SemaphoreType.DMA((flows,)),
            pltpu.SemaphoreType.DMA((flows,)),
            pltpu.SemaphoreType.DMA((CHUNKS,)),
            pltpu.SemaphoreType.DMA((2,)),
            pltpu.SemaphoreType.DMA((3,)),
        ],
        compiler_params=pltpu.CompilerParams(has_side_effects=True, vmem_limit_bytes=60 * 1024 * 1024),
    )(tokens, weight)
    return own, extra


def share_kernel(grp_count, tp_count, mine, out, held, send, recv, local):
    g = lax.axis_index("grp")
    t = lax.axis_index("tp")

    def copy(i, src, dst, device):
        return pltpu.make_async_remote_copy(
            src_ref=src, dst_ref=dst, send_sem=send.at[i], recv_sem=recv.at[i],
            device_id=device, device_id_type=pl.DeviceIdType.MESH,
        )

    own = pltpu.make_async_copy(mine, held.at[g, t], local)
    own.start()
    first = [copy(d - 1, mine, held.at[g, t], (g, t ^ d)) for d in range(1, tp_count)]
    for c in first:
        c.start()
    own.wait()
    for d in range(1, tp_count):
        copy(d - 1, mine, held.at[g, t ^ d], (g, t)).wait_recv()
    second = [
        copy(tp_count - 1 + d - 1, held.at[g], held.at[g], ((g + d) % grp_count, t))
        for d in range(1, grp_count)
    ]
    for c in second:
        c.start()
    for d in range(1, grp_count):
        source = held.at[(g + grp_count - d) % grp_count]
        copy(tp_count - 1 + d - 1, source, source, (g, t)).wait_recv()
    for c in first + second:
        c.wait_send()
    out[...] = held[...]


def share(mine, grp_count, tp_count):
    shape = (grp_count, tp_count) + mine.shape
    flows = grp_count + tp_count - 2
    return pl.pallas_call(
        functools.partial(share_kernel, grp_count, tp_count),
        in_specs=[pl.BlockSpec(memory_space=pl.ANY)],
        out_specs=pl.BlockSpec(memory_space=pltpu.VMEM),
        out_shape=jax.ShapeDtypeStruct(shape, mine.dtype),
        scratch_shapes=[
            pltpu.VMEM(shape, mine.dtype),
            pltpu.SemaphoreType.DMA((flows,)),
            pltpu.SemaphoreType.DMA((flows,)),
            pltpu.SemaphoreType.DMA,
        ],
        compiler_params=pltpu.CompilerParams(has_side_effects=True),
    )(mine)


def shards(tokens, joined_weight, rollout_lengths, prompt_of, score_weight):
    grp_count = lax.axis_size("grp")
    tp_count = lax.axis_size("tp")
    n = grp_count // CORES
    g = lax.axis_index("grp")
    z = g // CORES
    own, extra = project(tokens, joined_weight, n, tp_count)
    flag = ((z == 0) | (z == n - 1)).astype(jnp.int32).reshape(1)
    attention, reward = attend(own, extra, rollout_lengths, flag, score_weight)
    reward = reward / rollout_lengths.astype(jnp.float32)
    sent = jnp.stack([reward, prompt_of[:, 0].astype(jnp.float32)])
    count = reward.shape[0]
    sent = jnp.pad(sent, ((0, -2 % 8), (0, -count % 128)))
    gathered = share(sent, grp_count, tp_count)[:, :, :2, :count]
    everyone = jnp.sum(gathered[:, :, 0], axis=1).reshape(-1)
    prompts = gathered[:, 0, 1].reshape(-1, 1).astype(jnp.int32)
    labels = jnp.arange(grp_count)[None, :]
    onehot = (prompts == labels).astype(jnp.float32)
    counts = jnp.sum(onehot, axis=0)
    totals = jnp.sum(onehot * everyone[:, None], axis=0)
    squares = jnp.sum(onehot * (everyone * everyone)[:, None], axis=0)
    divisor = jnp.maximum(counts, 1.0)
    average = totals / divisor
    spread = squares / divisor - average * average
    mine = (prompt_of == labels).astype(jnp.float32)
    own_mean = jnp.sum(mine * average[None, :], axis=1)
    own_var = jnp.sum(mine * spread[None, :], axis=1)
    rewards = lax.dynamic_slice(everyone, (g * reward.shape[0],), reward.shape)
    advantages = (rewards - own_mean) / jnp.sqrt(own_var + 0.25)
    return (attention, advantages)


def solution(mesh):
    return jax.shard_map(
        shards,
        mesh=mesh,
        in_specs=(P("grp", None), P(("grp", "tp"), None), P("grp"), P("grp", None), P("tp")),
        out_specs=(P("grp", "tp"), P("grp")),
        check_vma=False,
    )
```

profile of v0, /device:TPU:0, one launch (start us, length us, event | category | flops | bytes accessed | tf_op | source)
XLA Modules:
  0.0 333.4 jit_solution(12010889512538608317)
XLA Ops:
  0.6 0.0 copy-start
  0.7 299.3 %shard_map.68 = (f32[5,1024,512]{2,1,0:T(8,128)}, bf16[5,1024,512]{2,1,0:T(8,128)(2,1)}, bf16[5,8192,512]{2,1,0:T(8,128)(2,1)}, bf16[1024,4096]{1,0:T(8,128)(2,1)}, bf16[5,1024,512]{2,1,0:T(8,128)(2,1)}) custom-call(bf16[1024,8192]{1,0:T(8,128)(2,1)} %tokens.1, bf16[256,10240]{1,0:T(8,128)(2,1)} %weight.1), custom_call_target="tpu_custom_call" | custom-call | tf_op jit(solution)/shard_map/pallas_call | solution.py:281
  300.0 0.0 copy-start.1
  300.0 0.0 copy-start.2
  300.0 0.0 copy-done
  300.0 0.6 reshape.57.weight_ref
  300.6 14.3 %shard_map.69 = (bf16[1024,2048]{1,0:T(8,128)(2,1)}, f32[8,8,128]{2,1,0:T(8,128)}) custom-call(s32[8]{0:T(128)} %lengths_ref.1, s32[1]{0:T(128)} %bitcast.flag_ref, bf16[1,2048]{1,0:T(2,128)(2,1)} %reshape.57.weight_ref, f32[5,1024,512]{2,1,0:T(8,128)} %get-tuple-element.6.own, bf16[5,1024,512]{2,1,0:T(8,128)(2,1)} %get-tuple-element.7.extra), custom_call_target="tpu_custom_call" | custom-call | tf_op jit(solution)/shard_map/pallas_call | solution.py:65
  314.9 0.9 slice_reduce_fusion.1
  315.8 0.0 copy-done.1
  315.8 0.0 copy-done.2
  315.8 0.6 select_maximum_fusion.mine
  316.4 14.2 %shard_map.70 = f32[8,4,8,128]{3,2,1,0:T(8,128)} custom-call(f32[8,128]{1,0:T(8,128)} %select_maximum_fusion.mine), custom_call_target="tpu_custom_call" | custom-call | tf_op jit(solution)/shard_map/pallas_call | solution.py:344
  330.6 0.9 slice_reduce_fusion
  331.5 0.1 reshape.58
  331.6 0.8 convert_reduce_fusion.1
  332.4 0.1 convert_element_type.38
  332.4 0.1 select_reduce_fusion.1
  332.6 0.2 select_reduce_fusion.2
  332.8 0.6 rsqrt_multiply_fusion
  (4 shorter events, 0.0 us)
Async XLA Ops:
  0.6 299.3 %copy-start = (bf16[2048]{0:T(1024)(128)(2,1)S(1)}, bf16[2048]{0:T(1024)(128)(2,1)}, u32[]{:S(2)}) copy-start(bf16[2048]{0:T(1024)(128)(2,1)} %param.9) | copy-start | bytes 12292
  300.0 15.8 %copy-start.1 = (s32[8]{0:T(128)S(1)}, s32[8]{0:T(128)}, u32[]{:S(2)}) copy-start(s32[8]{0:T(128)} %lengths_ref.1) | copy-start | bytes 100
  300.0 15.8 %copy-start.2 = (s32[8,1]{0,1:T(1,128)S(1)}, s32[8,1]{0,1:T(1,128)}, u32[]{:S(2)}) copy-start(s32[8,1]{0,1:T(1,128)} %param.8) | copy-start | bytes 100
where the time goes:
time: 334 us; the launch traced here: 333 us
  Pallas kernels  328 us (98%)
    pallas_call x1, Pallas kernels, project(): pl.pallas_call(functools.partial(project_kernel, n, tp_count), in_specs=[...  299 us
    pallas_call x1, Pallas kernels, attend(): pl.pallas_call(functools.partial(attend_kernel, features // (ratio * HEAD...  14.3 us
    pallas_call x1, Pallas kernels, share(): pl.pallas_call(functools.partial(share_kernel, grp_count, tp_count), in_s...  14.2 us

commit v1 on v0

--- a/solution.py
+++ b/solution.py
@@ -11,7 +11,8 @@
 KV_HEAD_COUNT = 8
 HEAD_SIZE = 128
 CORES = 2
-CHUNKS = 5
+WIDTH = 256
+SPLIT = 2
 
 
 def attend_kernel(groups, chunks, lengths_ref, flag_ref, weight_ref, own, extra, out_ref, reward_ref):
@@ -82,8 +83,8 @@
 
 
 def project_kernel(
-    n, tp_count, tokens, weight, own_out, extra, gath, far, prod,
-    tok_v, far_v, w_v, acc, pbuf, send, recv, loads, w_sem, misc,
+    n, tp_count, tokens, weight, own_out, extra, gath, far,
+    tok_v, far_v, w_v, acc, pbuf, send, recv, loads, w_sem, outs, misc,
 ):
     g = lax.axis_index("grp")
     t = lax.axis_index("tp")
@@ -97,38 +98,61 @@
     part = rows // tp_count
     far_cols = far.shape[1]
     steps = n - 2
+    end_steps = n // 2 - 1
+    left = z < n // 2
+    sign = jnp.where(left, 1, -1)
+    is_end = (z == 0) | (z == n - 1)
     inner = (z >= 1) & (z <= n - 2)
     helper = (z == 1) | (z == n - 2)
-    at_end = (z == 0) | (z == n - 1)
-    first_far = jnp.where(z < n // 2, 2, 0)
-    ids = {}
-
-    def sem(key):
-        return ids.setdefault(key, len(ids))
-
-    def remote(key, src, dst, device):
-        i = sem(key)
+    first_far = jnp.where(left, 2, 0)
+    always = z >= 0
+    mid_device = (g + sign * CORES, t)
+    end_device = (g - sign * CORES, t)
+    sibling = (g + 1 - 2 * core, t)
+    end_inner = jnp.where(left, z >= 2, z <= n - 3)
+    table = {}
+    used = [0]
+
+    def base(key, size):
+        if key not in table:
+            table[key] = used[0]
+            used[0] += size
+        return table[key]
+
+    def flow(side, s):
+        forth, back = base(("right", s), chunks), base(("left", s), chunks)
+        return jnp.where(left, back, forth) if side == "mid" else jnp.where(left, forth, back)
+
+    def local(key):
+        return base(key, chunks)
+
+    def remote(i, src, dst, device):
         return pltpu.make_async_remote_copy(
             src_ref=src, dst_ref=dst, send_sem=send.at[i], recv_sem=recv.at[i],
             device_id=device, device_id_type=pl.DeviceIdType.MESH,
         )
 
-    sends = []
-
-    def start(cond, key, src, dst, device):
+    def start(cond, i, src, dst, device):
         @pl.when(cond)
         def _():
-            remote(key, src, dst, device).start()
-
-        sends.append((cond, key, src, dst, device))
-
-    def arrived(cond, key, dst):
+            remote(i, src, dst, device).start()
+
+    def arrived(cond, i, dst):
         @pl.when(cond)
         def _():
-            remote(key, dst, dst, (g, t)).wait_recv()
-
-    always = z >= 0
-    sibling = (g + 1 - 2 * core, t)
+            remote(i, dst, dst, (g, t)).wait_recv()
+
+    def sent(cond, i, src):
+        @pl.when(cond)
+        def _():
+            remote(i, src, src, (g, t)).wait_send()
+
+    def each(count, body):
+        def step(q, carry):
+            body(q)
+            return carry
+
+        lax.fori_loop(0, count, step, 0)
 
     def piece(q, who):
         return gath.at[q, pl.ds(pl.multiple_of(z * plane + core * half + who * own_rows, own_rows), own_rows)]
@@ -139,167 +163,263 @@
     def columns_of(who, q):
         return weight.at[:, pl.ds(pl.multiple_of(who * columns + q * width, width), width)]
 
+    def has(side, s):
+        if side == "end":
+            return jnp.where(left, z - s >= 0, z + s <= n - 1)
+        reach = jnp.where(left, z + s <= n - 1, z - s >= 0)
+        return reach if s == 1 else reach & inner
+
+    def plane_of(side, s):
+        return jnp.clip(z + sign * s if side == "mid" else z - sign * s, 0, n - 1)
+
+    def own_copy(q):
+        return pltpu.make_async_copy(columns_of(t, q), piece(q, t), loads.at[q])
+
     def scatter(q):
-        pltpu.make_async_copy(columns_of(t, q), piece(q, t), loads.at[q]).start()
+        own_copy(q).start()
         for d in range(1, tp_count):
-            start(always, ("a", q, d), columns_of(t ^ d, q), piece(q, t), (g, t ^ d))
-
-    def gathered(q):
-        pltpu.make_async_copy(columns_of(t, q), piece(q, t), loads.at[q]).wait()
+            start(always, local(("a", d)) + q, columns_of(t ^ d, q), piece(q, t), (g, t ^ d))
+
+    def outward(q, src, dst):
+        start(always, flow("end", 1) + q, src, dst, mid_device)
+        start(inner, flow("mid", 1) + q, src, dst, end_device)
+
+    def gathered(q, split):
         for d in range(1, tp_count):
-            arrived(always, ("a", q, d), piece(q, t ^ d))
-
-    def launch(q):
+            arrived(always, local(("a", d)) + q, piece(q, t ^ d))
+            if split:
+                outward(q, piece(q, t ^ d), piece(q, t ^ d))
+        own_copy(q).wait()
         mine = block(q, z, core)
-        start(z >= 1, ("l", q, 1), mine, mine, (g - CORES, t))
-        start(z <= n - 2, ("r", q, 1), mine, mine, (g + CORES, t))
-        start(always, ("s", q), mine, mine, sibling)
-
-    def has(side, s):
-        reach = (z + s <= n - 1) if side == "l" else (z - s >= 0)
-        return reach if s == 1 else reach & inner
-
-    def forward(q, s):
-        for side, sign in (("l", 1), ("r", -1)):
-            here = jnp.clip(z + sign * s, 0, n - 1)
-            got = block(q, here, core)
-            arrived(has(side, s), (side, q, s), got)
-            if s < steps:
-                more = (z >= 2) if side == "l" else (z <= n - 3)
-                start(has(side, s) & more, (side, q, s + 1), got, got, (g - sign * CORES, t))
-            start(has(side, s), ("s" + side, q, s), got, got, sibling)
-
-    def swapped(q):
-        arrived(always, ("s", q), block(q, z, 1 - core))
-        for s in range(1, steps + 1):
-            for side, sign in (("l", 1), ("r", -1)):
-                here = jnp.clip(z + sign * s, 0, n - 1)
-                arrived(has(side, s), ("s" + side, q, s), block(q, here, 1 - core))
+        if not split:
+            outward(q, mine, mine)
+        start(always, local("s") + q, mine, mine, sibling)
+
+    def handle(side, s, q):
+        here = plane_of(side, s)
+        got = block(q, here, core)
+        there = has(side, s)
+        arrived(there, flow(side, s) + q, got)
+        if s < steps:
+            if side == "end":
+                start(there, flow(side, s + 1) + q, got, got, mid_device)
+            else:
+                start(there & end_inner, flow(side, s + 1) + q, got, got, end_device)
+        start(there, local((side, s)) + q, got, got, sibling)
+
+    def swapped(side, s, q):
+        arrived(has(side, s), local((side, s)) + q, block(q, plane_of(side, s), 1 - core))
+
+    def load(slot, q, p):
+        return pltpu.make_async_copy(
+            gath.at[q, pl.ds(pl.multiple_of(p * plane, plane), plane)], w_v.at[slot], w_sem.at[slot]
+        )
 
     tile = 256
 
-    def gemm(q, lhs, low, high, origin):
-        def load(p):
-            return pltpu.make_async_copy(
-                gath.at[q, pl.ds(pl.multiple_of(p * plane, plane), plane)], w_v.at[p % 2], w_sem.at[p % 2]
-            )
-
-        load(low).start()
-        acc[...] = jnp.zeros_like(acc)
-
-        def step(p, carry):
-            @pl.when(p + 1 < high)
-            def _():
-                load(p + 1).start()
-
-            load(p).wait()
-            cols = pl.ds(pl.multiple_of((p - origin) * plane, plane), plane)
-
-            def rows_step(m, carry):
-                at = pl.ds(pl.multiple_of(m * tile, tile), tile)
-                acc[at, :] += jnp.dot(lhs[at, cols], w_v[p % 2], preferred_element_type=jnp.float32)
-                return carry
-
-            return lax.fori_loop(0, rows // tile, rows_step, carry)
-
-        lax.fori_loop(low, high, step, 0)
-
-    def compute(q):
-        low = jnp.where(z == n - 1, n - 2, 0)
-        high = jnp.where(z == 0, 2, n)
-        gemm(q, tok_v, low, high, 0)
-        out = pltpu.make_async_copy(acc, own_out.at[q], misc.at[1])
-        out.start()
-        out.wait()
-
-    def assist(q):
-        @pl.when(helper)
-        def _():
-            gemm(q, far_v, first_far, first_far + steps, first_far)
-            pbuf[...] = acc[...].astype(pbuf.dtype)
-            out = pltpu.make_async_copy(pbuf, prod.at[q], misc.at[2])
-            out.start()
-            out.wait()
-
-        start(helper, ("p", q), prod.at[q], extra.at[q], (jnp.where(z == 1, g - CORES, g + CORES), t))
+    def over_rows(body):
+        each(rows // tile, lambda m: body(pl.ds(pl.multiple_of(m * tile, tile), tile)))
+
+    def columns_at(p):
+        return pl.ds(pl.multiple_of(p * plane, plane), plane)
+
+    def gemm(slot, q, p, fresh):
+        def body(at):
+            product = jnp.dot(tok_v[at, columns_at(p)], w_v[slot], preferred_element_type=jnp.float32)
+            if fresh:
+                acc[q, at, :] = product
+            else:
+                acc[q, at, :] += product
+
+        over_rows(body)
 
     def token_rows(who):
         return far.at[pl.ds(pl.multiple_of(who * part, part), part)]
 
+    def far_source(who):
+        return tokens.at[
+            pl.ds(pl.multiple_of(who * part, part), part),
+            pl.ds(pl.multiple_of(first_far * plane, plane), far_cols),
+        ]
+
+    twin = tp_count - 1
     load_tokens = pltpu.make_async_copy(tokens, tok_v, misc.at[0])
-    far_source = tokens.at[
-        pl.ds(pl.multiple_of(t * part, part), part),
-        pl.ds(pl.multiple_of(first_far * plane, plane), far_cols),
-    ]
-    start(at_end, ("t",), far_source, token_rows(t), (jnp.where(z == 0, g + CORES, g - CORES), t))
-    for q in range(chunks):
+    fill = pltpu.make_async_copy(far, far_v, misc.at[1])
+    start(is_end, base("t0", 1), far_source(t), token_rows(t), mid_device)
+    start(is_end, base("t1", 1), far_source(t ^ twin), token_rows(t ^ twin), mid_device)
+    for q in range(SPLIT):
         scatter(q)
+        outward(q, columns_of(t, q), piece(q, t))
+    each(chunks - SPLIT, lambda q: scatter(q + SPLIT))
     load_tokens.start()
-    for q in range(chunks):
-        gathered(q)
-        launch(q)
-    arrived(helper, ("t",), token_rows(t))
-    for d in range(1, tp_count):
-        start(helper, ("g", d), token_rows(t), token_rows(t), (g, t ^ d))
+    for q in range(SPLIT):
+        gathered(q, True)
+    each(chunks - SPLIT, lambda q: gathered(q + SPLIT, False))
+    arrived(helper, base("t0", 1), token_rows(t))
+    for d in range(1, twin):
+        start(helper, base(("g", d), 1), token_rows(t), token_rows(t), (g, t ^ d))
     load_tokens.wait()
-    for q in range(chunks - 1):
-        forward(q, 1)
-    for q in range(chunks):
+
+    def own_half(q):
+        arrived(always, local("s") + q, block(q, z, 1 - core))
+        load(q % 2, q, z).start()
+
+    own_half(0)
+
+    def own_step(q):
+        @pl.when(q + 1 < chunks)
+        def _():
+            own_half(q + 1)
+
+        load(q % 2, q, z).wait()
+        gemm(q % 2, q, z, True)
+
+    each(chunks, own_step)
+
+    def near_step(q):
+        @pl.when(q == chunks - 1)
+        def _():
+            handle("end", 1, 0)
+
+        handle("mid", 1, q)
+        swapped("mid", 1, q)
+        p = plane_of("mid", 1)
+        load(0, q, p).start()
+        load(0, q, p).wait()
+        gemm(0, q, p, False)
+
+    each(chunks, near_step)
+    arrived(helper, base("t1", 1), token_rows(t ^ twin))
+    for d in range(1, twin):
+        arrived(helper, base(("g", d), 1), token_rows(t ^ d))
+
+    @pl.when(helper)
+    def _():
+        fill.start()
+        load(0, 0, plane_of("mid", 1)).start()
+        fill.wait()
+
+    others = [("mid", s) for s in range(2, steps + 1)] + [("end", s) for s in range(1, end_steps + 1)]
+    slot_of = {("mid", 1): 0}
+    for other in others:
+        slot_of[other] = len(slot_of)
+
+    def product(q):
+        return pbuf.at[q % 2]
+
+    def last_step(q):
+        @pl.when(q + 1 < chunks)
+        def _():
+            handle("end", 1, q + 1)
+
         for s in range(2, steps + 1):
-            forward(q, s)
-        swapped(q)
-        if q == 0:
-            for d in range(1, tp_count):
-                arrived(helper, ("g", d), token_rows(t ^ d))
-
-            @pl.when(helper)
+            if s <= end_steps:
+                handle("end", s, q)
+            handle("mid", s, q)
+        for side, s in others:
+            swapped(side, s, q)
+
+            @pl.when(has(side, s))
             def _():
-                fill = pltpu.make_async_copy(far, far_v, misc.at[0])
-                fill.start()
-                fill.wait()
-
-        assist(q)
-        if q == 0:
-            forward(chunks - 1, 1)
-        compute(q)
-    for q in range(chunks):
-        arrived(at_end, ("p", q), extra.at[q])
-    for cond, key, src, dst, device in sends:
-        @pl.when(cond)
-        def _():
-            remote(key, src, dst, device).wait_send()
+                load(slot_of[side, s], q, plane_of(side, s)).start()
+
+        for side, s in others:
+            @pl.when(has(side, s))
+            def _():
+                load(slot_of[side, s], q, plane_of(side, s)).wait()
+
+        @pl.when(helper)
+        def _():
+            load(0, q, plane_of("mid", 1)).wait()
+
+            @pl.when(q >= 2)
+            def _():
+                sent(always, local("p") + q - 2, product(q))
+
+            def body(at):
+                total = None
+                for s in range(1, steps + 1):
+                    cols = columns_at(plane_of("mid", s) - first_far)
+                    term = jnp.dot(
+                        far_v[at, cols], w_v[slot_of["mid", s]], preferred_element_type=jnp.float32
+                    )
+                    total = term if total is None else total + term
+                pbuf[q % 2, at, :] = total.astype(pbuf.dtype)
+
+            over_rows(body)
+            remote(local("p") + q, product(q), extra.at[q], end_device).start()
+
+            @pl.when(q + 1 < chunks)
+            def _():
+                load(0, q + 1, plane_of("mid", 1)).start()
+
+        for side, s in others:
+            @pl.when(has(side, s))
+            def _():
+                gemm(slot_of[side, s], q, plane_of(side, s), False)
+
+        pltpu.make_async_copy(acc.at[q], own_out.at[q], outs.at[q]).start()
+
+    each(chunks, last_step)
+
+    def finish(q):
+        arrived(is_end, local("p") + q, extra.at[q])
+        pltpu.make_async_copy(acc.at[q], own_out.at[q], outs.at[q]).wait()
+        mine = block(q, z, core)
+        for d in range(1, tp_count):
+            sent(always, local(("a", d)) + q, piece(q, t))
+        sent(always, flow("end", 1) + q, mine)
+        sent(inner, flow("mid", 1) + q, mine)
+        sent(always, local("s") + q, mine)
+        for side, count in (("end", end_steps), ("mid", steps)):
+            for s in range(1, count + 1):
+                there = has(side, s)
+                if s < steps:
+                    sent(there if side == "end" else there & end_inner, flow(side, s + 1) + q, mine)
+                sent(there, local((side, s)) + q, mine)
+
+    each(chunks, finish)
+    for q in range(max(chunks - 2, 0), chunks):
+        sent(helper, local("p") + q, product(q))
+    sent(is_end, base("t0", 1), token_rows(t))
+    sent(is_end, base("t1", 1), token_rows(t))
+    for d in range(1, twin):
+        sent(helper, base(("g", d), 1), token_rows(t))
 
 
 def project(tokens, weight, n, tp_count):
     rows, depth = tokens.shape
     own_rows = weight.shape[0]
-    width = weight.shape[1] // tp_count // CHUNKS
+    width = WIDTH
+    chunks = weight.shape[1] // tp_count // width
     plane = own_rows * tp_count * CORES
     far = plane * (n - 2)
-    flows = CHUNKS * (tp_count + 1 + 4 * (n - 2)) + tp_count
+    steps, end_steps = n - 2, n // 2 - 1
+    flows = chunks * (tp_count + 1 + 3 * steps + end_steps) + tp_count
+    slots = steps + end_steps
     anywhere = pl.BlockSpec(memory_space=pl.ANY)
     own, extra, *_ = pl.pallas_call(
         functools.partial(project_kernel, n, tp_count),
         in_specs=[anywhere] * 2,
-        out_specs=[anywhere] * 5,
+        out_specs=[anywhere] * 4,
         out_shape=[
-            jax.ShapeDtypeStruct((CHUNKS, rows, width), jnp.float32),
-            jax.ShapeDtypeStruct((CHUNKS, rows, width), jnp.bfloat16),
-            jax.ShapeDtypeStruct((CHUNKS, depth, width), jnp.bfloat16),
+            jax.ShapeDtypeStruct((chunks, rows, width), jnp.float32),
+            jax.ShapeDtypeStruct((chunks, rows, width), jnp.bfloat16),
+            jax.ShapeDtypeStruct((chunks, depth, width), jnp.bfloat16),
             jax.ShapeDtypeStruct((rows, far), jnp.bfloat16),
-            jax.ShapeDtypeStruct((CHUNKS, rows, width), jnp.bfloat16),
         ],
         scratch_shapes=[
             pltpu.VMEM((rows, depth), jnp.bfloat16),
             pltpu.VMEM((rows, far), jnp.bfloat16),
-            pltpu.VMEM((2, plane, width), jnp.bfloat16),
-            pltpu.VMEM((rows, width), jnp.float32),
-            pltpu.VMEM((rows, width), jnp.bfloat16),
+            pltpu.VMEM((slots, plane, width), jnp.bfloat16),
+            pltpu.VMEM((chunks, rows, width), jnp.float32),
+            pltpu.VMEM((2, rows, width), jnp.bfloat16),
             pltpu.SemaphoreType.DMA((flows,)),
             pltpu.SemaphoreType.DMA((flows,)),
-            pltpu.SemaphoreType.DMA((CHUNKS,)),
+            pltpu.SemaphoreType.DMA((chunks,)),
+            pltpu.SemaphoreType.DMA((slots,)),
+            pltpu.SemaphoreType.DMA((chunks,)),
             pltpu.SemaphoreType.DMA((2,)),
-            pltpu.SemaphoreType.DMA((3,)),
         ],
         compiler_params=pltpu.CompilerParams(has_side_effects=True, vmem_limit_bytes=60 * 1024 * 1024),
     )(tokens, weight)

time: 334 us -> 307 us (0.919)
  Pallas kernels: 328 us -> 300 us
    pallas_call x1, Pallas kernels: 299 us -> 274 us  [project(): pl.pallas_call(functools.partial(project_kernel, n, tp_count), in_specs=[...]
where the time goes in v1:
time: 307 us; the launch traced here: 306 us
  Pallas kernels  300 us (98%)
  other arithmetic  3.25 us (1%)
    pallas_call x1, Pallas kernels, project(): pl.pallas_call(functools.partial(project_kernel, n, tp_count), in_specs=[...  274 us
    pallas_call x1, Pallas kernels, attend(): pl.pallas_call(functools.partial(attend_kernel, features // (ratio * HEAD...  14.3 us
    pallas_call x1, Pallas kernels, share(): pl.pallas_call(functools.partial(share_kernel, grp_count, tp_count), in_s...  12.2 us

profile of v1, /device:TPU:0, one launch (start us, length us, event | category | flops | bytes accessed | tf_op | source)
XLA Modules:
  0.0 305.7 jit_solution(12254747077133255256)
XLA Ops:
  0.6 0.0 copy-start
  0.7 273.6 %shard_map.68 = (f32[10,1024,256]{2,1,0:T(8,128)}, bf16[10,1024,256]{2,1,0:T(8,128)(2,1)}, bf16[10,8192,256]{2,1,0:T(8,128)(2,1)}, bf16[1024,4096]{1,0:T(8,128)(2,1)}) custom-call(bf16[1024,8192]{1,0:T(8,128)(2,1)} %tokens.1, bf16[256,10240]{1,0:T(8,128)(2,1)} %weight.1), custom_call_target="tpu_custom_call" | custom-call | tf_op jit(solution)/shard_map/pallas_call | solution.py:401
  274.2 0.0 copy-start.1
  274.2 0.0 copy-start.2
  274.3 0.0 copy-done
  274.3 0.6 reshape.57.weight_ref
  274.9 14.3 %shard_map.69 = (bf16[1024,2048]{1,0:T(8,128)(2,1)}, f32[8,8,128]{2,1,0:T(8,128)}) custom-call(s32[8]{0:T(128)} %lengths_ref.1, s32[1]{0:T(128)} %bitcast.flag_ref, bf16[1,2048]{1,0:T(2,128)(2,1)} %reshape.57.weight_ref, f32[10,1024,256]{2,1,0:T(8,128)} %get-tuple-element.6.own, bf16[10,1024,256]{2,1,0:T(8,128)(2,1)} %get-tuple-element.7.extra), custom_call_target="tpu_custom_call" | custom-call | tf_op jit(solution)/shard_map/pallas_call | solution.py:66
  289.1 0.9 slice_reduce_fusion.1
  290.1 0.0 copy-done.1
  290.1 0.0 copy-done.2
  290.1 0.6 select_maximum_fusion.mine
  290.7 12.2 %shard_map.70 = f32[8,4,8,128]{3,2,1,0:T(8,128)} custom-call(f32[8,128]{1,0:T(8,128)} %select_maximum_fusion.mine), custom_call_target="tpu_custom_call" | custom-call | tf_op jit(solution)/shard_map/pallas_call | solution.py:464
  302.9 0.9 slice_reduce_fusion
  303.8 0.1 reshape.58
  303.9 0.8 convert_reduce_fusion.1
  304.7 0.1 convert_element_type.38
  304.7 0.1 select_reduce_fusion.1
  304.9 0.2 select_reduce_fusion.2
  305.1 0.6 rsqrt_multiply_fusion
  (4 shorter events, 0.0 us)
Async XLA Ops:
  0.6 273.6 %copy-start = (bf16[2048]{0:T(1024)(128)(2,1)S(1)}, bf16[2048]{0:T(1024)(128)(2,1)}, u32[]{:S(2)}) copy-start(bf16[2048]{0:T(1024)(128)(2,1)} %param.9) | copy-start | bytes 12292
  274.2 15.8 %copy-start.1 = (s32[8]{0:T(128)S(1)}, s32[8]{0:T(128)}, u32[]{:S(2)}) copy-start(s32[8]{0:T(128)} %lengths_ref.1) | copy-start | bytes 100
  274.2 15.8 %copy-start.2 = (s32[8,1]{0,1:T(1,128)S(1)}, s32[8,1]{0,1:T(1,128)}, u32[]{:S(2)}) copy-start(s32[8,1]{0,1:T(1,128)} %param.8) | copy-start | bytes 100

commit v2 on v1

v2 whole, which is shorter than its diff:
```python
import functools

import jax
import jax.numpy as jnp
from jax import lax
from jax.experimental import pallas as pl
from jax.experimental.pallas import tpu as pltpu
from jax.sharding import PartitionSpec as P

QUERY_HEADS = 64
KV_HEAD_COUNT = 8
HEAD_SIZE = 128
CORES = 2
WIDTH = 256
SPLIT = 2


def fused_kernel(
    n, tp_count, lengths, spans, prompts, score, tokens, weight, attention, advantages, gath, far,
    tok_v, far_v, w_v, acc, pbuf, extra, kv, mixed_v, total, tp_held, grp_held, share_v,
    send, recv, loads, w_sem, outs, misc,
):
    g = lax.axis_index("grp")
    t = lax.axis_index("tp")
    z, core = g // CORES, g % CORES
    rows, depth = tokens.shape
    chunks, _, width = gath.shape
    own_rows = weight.shape[0]
    half = own_rows * tp_count
    plane = half * CORES
    columns = width * chunks
    part = rows // tp_count
    far_cols = far.shape[1]
    steps = n - 2
    end_steps = n // 2 - 1
    left = z < n // 2
    sign = jnp.where(left, 1, -1)
    is_end = (z == 0) | (z == n - 1)
    inner = (z >= 1) & (z <= n - 2)
    helper = (z == 1) | (z == n - 2)
    first_far = jnp.where(left, 2, 0)
    always = z >= 0
    mid_device = (g + sign * CORES, t)
    end_device = (g - sign * CORES, t)
    sibling = (g + 1 - 2 * core, t)
    end_inner = jnp.where(left, z >= 2, z <= n - 3)
    table = {}
    used = [0]

    def base(key, size):
        if key not in table:
            table[key] = used[0]
            used[0] += size
        return table[key]

    def flow(side, s):
        forth, back = base(("right", s), chunks + 1), base(("left", s), chunks + 1)
        return jnp.where(left, back, forth) if side == "mid" else jnp.where(left, forth, back)

    def local(key):
        return base(key, chunks + 1)

    def remote(i, src, dst, device):
        return pltpu.make_async_remote_copy(
            src_ref=src, dst_ref=dst, send_sem=send.at[i], recv_sem=recv.at[i],
            device_id=device, device_id_type=pl.DeviceIdType.MESH,
        )

    def start(cond, i, src, dst, device):
        @pl.when(cond)
        def _():
            remote(i, src, dst, device).start()

    def arrived(cond, i, dst):
        @pl.when(cond)
        def _():
            remote(i, dst, dst, (g, t)).wait_recv()

    def sent(cond, i, src):
        @pl.when(cond)
        def _():
            remote(i, src, src, (g, t)).wait_send()

    def each(count, body):
        def step(q, carry):
            body(q)
            return carry

        lax.fori_loop(0, count, step, 0)

    def piece(q, who):
        return gath.at[q, pl.ds(pl.multiple_of(z * plane + core * half + who * own_rows, own_rows), own_rows)]

    last = chunks - 1
    narrow = width // 2

    def span(h):
        return slice(None) if h is None else slice(h * narrow, (h + 1) * narrow)

    def step_of(q, h):
        return q if h is None else q + h

    def block(q, p, c, h=None):
        return gath.at[q, pl.ds(pl.multiple_of(p * plane + c * half, half), half), span(h)]

    ratio = QUERY_HEADS // KV_HEAD_COUNT
    heads = width // HEAD_SIZE
    per_group = (ratio + 2) // heads

    def columns_of(who, q):
        at = who * columns + (q // per_group * per_group + (q + per_group - 1) % per_group) * width
        return weight.at[:, pl.ds(pl.multiple_of(at, width), width)]

    def has(side, s):
        if side == "end":
            return jnp.where(left, z - s >= 0, z + s <= n - 1)
        reach = jnp.where(left, z + s <= n - 1, z - s >= 0)
        return reach if s == 1 else reach & inner

    def plane_of(side, s):
        return jnp.clip(z + sign * s if side == "mid" else z - sign * s, 0, n - 1)

    def own_copy(q):
        return pltpu.make_async_copy(columns_of(t, q), piece(q, t), loads.at[q])

    def scatter(q):
        own_copy(q).start()
        for d in range(1, tp_count):
            start(always, local(("a", d)) + q, columns_of(t ^ d, q), piece(q, t), (g, t ^ d))

    def outward(q, src, dst):
        start(always, flow("end", 1) + q, src, dst, mid_device)
        start(inner, flow("mid", 1) + q, src, dst, end_device)

    def gathered(q, split):
        for d in range(1, tp_count):
            arrived(always, local(("a", d)) + q, piece(q, t ^ d))
            if split:
                outward(q, piece(q, t ^ d), piece(q, t ^ d))
        own_copy(q).wait()
        mine = block(q, z, core)
        if not split:
            outward(q, mine, mine)
        start(always, local("s") + q, mine, mine, sibling)

    def onward(side, s, q, h):
        got = block(q, plane_of(side, s), core, h)
        at = flow(side, s + 1) + step_of(q, h)
        if side == "end":
            start(has(side, s), at, got, got, mid_device)
        else:
            start(has(side, s) & end_inner, at, got, got, end_device)

    def handle(side, s, q, h=None):
        got = block(q, plane_of(side, s), core, h)
        arrived(has(side, s), flow(side, s) + step_of(q, h), got)
        if s < steps and s == 1:
            @pl.when(q < last)
            def _():
                onward(side, s, q, None)

            @pl.when(q == last)
            def _():
                onward(side, s, last, 0)
                onward(side, s, last, 1)

        elif s < steps:
            onward(side, s, q, h)
        start(has(side, s), local((side, s)) + step_of(q, h), got, got, sibling)

    def swapped(side, s, q, h=None):
        arrived(has(side, s), local((side, s)) + step_of(q, h), block(q, plane_of(side, s), 1 - core, h))

    def load(slot, q, p, h=None):
        return pltpu.make_async_copy(
            gath.at[q, pl.ds(pl.multiple_of(p * plane, plane), plane), span(h)],
            w_v.at[slot, :, span(h)], w_sem.at[slot],
        )

    def columns_at(p):
        return pl.ds(pl.multiple_of(p * plane, plane), plane)

    def gemm(slot, q, p, fresh, h=None):
        result = jnp.dot(tok_v[:, columns_at(p)], w_v[slot, :, span(h)], preferred_element_type=jnp.float32)
        if fresh:
            acc[q] = result
        else:
            acc[q, :, span(h)] += result

    def token_rows(who):
        return far.at[pl.ds(pl.multiple_of(who * part, part), part)]

    def far_source(who):
        return tokens.at[
            pl.ds(pl.multiple_of(who * part, part), part),
            pl.ds(pl.multiple_of(first_far * plane, plane), far_cols),
        ]

    twin = tp_count - 1
    load_tokens = pltpu.make_async_copy(tokens, tok_v, misc.at[0])
    fill = pltpu.make_async_copy(far, far_v, misc.at[1])
    start(is_end, base("t0", 1), far_source(t), token_rows(t), mid_device)
    start(is_end, base("t1", 1), far_source(t ^ twin), token_rows(t ^ twin), mid_device)
    for q in range(SPLIT):
        scatter(q)
        outward(q, columns_of(t, q), piece(q, t))
    each(chunks - SPLIT, lambda q: scatter(q + SPLIT))
    load_tokens.start()
    for q in range(SPLIT):
        gathered(q, True)
    each(chunks - SPLIT, lambda q: gathered(q + SPLIT, False))
    arrived(helper, base("t0", 1), token_rows(t))
    for d in range(1, twin):
        start(helper, base(("g", d), 1), token_rows(t), token_rows(t), (g, t ^ d))
    load_tokens.wait()

    def own_half(q):
        arrived(always, local("s") + q, block(q, z, 1 - core))
        load(q % 2, q, z).start()

    own_half(0)

    def own_step(q):
        @pl.when(q + 1 < chunks)
        def _():
            own_half(q + 1)

        load(q % 2, q, z).wait()
        gemm(q % 2, q, z, True)

    each(chunks, own_step)

    def near_step(q):
        @pl.when(q == chunks - 1)
        def _():
            handle("end", 1, 0)

        handle("mid", 1, q)
        swapped("mid", 1, q)
        p = plane_of("mid", 1)
        load(0, q, p).start()
        load(0, q, p).wait()
        gemm(0, q, p, False)

    each(chunks, near_step)
    if chunks > 1:
        handle("end", 1, 1)
    arrived(helper, base("t1", 1), token_rows(t ^ twin))
    for d in range(1, twin):
        arrived(helper, base(("g", d), 1), token_rows(t ^ d))

    @pl.when(helper)
    def _():
        fill.start()
        load(0, 0, plane_of("mid", 1)).start()
        fill.wait()

    others = [("mid", s) for s in range(2, steps + 1)] + [("end", s) for s in range(1, end_steps + 1)]
    slot_of = {("mid", 1): 0}
    for other in others:
        slot_of[other] = len(slot_of)

    def product(q, h=None):
        return pbuf.at[step_of(q, h) % 2, :, span(h)]

    def retire(q):
        mine = block(q, z, core)
        for d in range(1, tp_count):
            sent(always, local(("a", d)) + q, piece(q, t))
        sent(always, flow("end", 1) + q, mine)
        sent(inner, flow("mid", 1) + q, mine)
        sent(always, local("s") + q, mine)
        for side in ("end", "mid"):
            sent(has(side, 1), local((side, 1)) + q, mine)

    def retire_far(q, h=None):
        mine = block(q, z, core, h)
        at = step_of(q, h)
        for side, count in (("end", end_steps), ("mid", steps)):
            for s in range(1, count + 1):
                if s < steps:
                    there = has(side, s)
                    sent(there if side == "end" else there & end_inner, flow(side, s + 1) + at, mine)
                if s > 1:
                    sent(has(side, s), local((side, s)) + at, mine)

    slot = rows // lengths.shape[0]
    rollouts = lengths.shape[0]
    s_pos = lax.broadcasted_iota(jnp.int32, (slot, slot), 0)
    t_pos = lax.broadcasted_iota(jnp.int32, (slot, slot), 1)

    def rows_of(r):
        return slice(r * slot, (r + 1) * slot)

    def out_index(q):
        return q // per_group * (per_group - 1) + q % per_group - 1

    def out_copy(q, h=None):
        index = out_index(q)
        at = index * width if h is None else index * width + h * narrow
        count = width if h is None else narrow
        cols = pl.ds(pl.multiple_of(at, HEAD_SIZE), count)
        which = index % 2 if h != 1 else 2
        return pltpu.make_async_copy(mixed_v.at[index % 2, :, span(h)], attention.at[:, cols], outs.at[which])

    def attend(q, h=None):
        index = out_index(q)
        if h is None:
            @pl.when(index >= 2)
            def _():
                out_copy(q).wait()

        elif h == 0:
            out_copy(q).wait()
        members = range(heads) if h is None else range(h * heads // 2, (h + 1) * heads // 2)
        weights = score[pl.ds(index, 1), :]
        for r in range(rollouts):
            at = rows_of(r)
            allowed = ((t_pos <= s_pos) & (t_pos < lengths[r]))[None]
            joined = acc[q, at, span(h)].astype(jnp.bfloat16)
            count = len(members)
            queries = jnp.concatenate(
                [joined[:, a * HEAD_SIZE : (a + 1) * HEAD_SIZE] for a in range(count)], axis=0
            )
            scores = lax.dot_general(
                queries, kv[at, :HEAD_SIZE], (((1,), (1,)), ((), ())), preferred_element_type=jnp.float32
            ) * HEAD_SIZE ** (-0.5)
            scores = jnp.where(allowed, scores.reshape(count, slot, slot), jnp.float32(-1e30))
            expo = jnp.exp(scores - jnp.max(scores, axis=-1, keepdims=True))
            probs = expo * (1.0 / jnp.sum(expo, axis=-1, keepdims=True))
            probs = probs.astype(jnp.bfloat16).reshape(count * slot, slot)
            mixed = jnp.dot(probs, kv[at, HEAD_SIZE:], preferred_element_type=jnp.float32).astype(jnp.bfloat16)
            summed = total[at, :]
            for i, a in enumerate(members):
                part_out = mixed[i * slot : (i + 1) * slot]
                cols = slice(a * HEAD_SIZE, (a + 1) * HEAD_SIZE)
                mixed_v[index % 2, at, cols] = part_out
                summed += part_out.astype(jnp.float32) * weights[:, cols]
            total[at, :] = summed
        out_copy(q, h).start()

    total[...] = jnp.zeros_like(total)

    def far_step(q, h=None):
        step = step_of(q, h)
        for s in range(2, steps + 1):
            if s <= end_steps:
                handle("end", s, q, h)
            handle("mid", s, q, h)
        for side, s in others:
            if s > 1 or h != 1:
                swapped(side, s, q, h if s > 1 else None)

            @pl.when(has(side, s))
            def _():
                load(slot_of[side, s], q, plane_of(side, s), h).start()

        for side, s in others:
            @pl.when(has(side, s))
            def _():
                load(slot_of[side, s], q, plane_of(side, s), h).wait()

        @pl.when(helper)
        def _():
            if h != 1:
                load(0, q, plane_of("mid", 1)).wait()

            @pl.when(step >= 2)
            def _():
                sent(always, local("p") + step - 2, pbuf.at[step % 2])

            whole = None
            for s in range(1, steps + 1):
                cols = columns_at(plane_of("mid", s) - first_far)
                term = jnp.dot(
                    far_v[:, cols], w_v[slot_of["mid", s], :, span(h)], preferred_element_type=jnp.float32
                )
                whole = term if whole is None else whole + term
            pbuf[step % 2, :, span(h)] = whole.astype(pbuf.dtype)
            remote(local("p") + step, product(q, h), extra.at[q, :, span(h)], end_device).start()
            if h is None:
                load(0, q + 1, plane_of("mid", 1)).start()

        if h is None:
            @pl.when(q + 2 < chunks)
            def _():
                handle("end", 1, q + 2)

        for side, s in others:
            @pl.when(has(side, s))
            def _():
                gemm(slot_of[side, s], q, plane_of(side, s), False, h)

        arrived(is_end, local("p") + step, extra.at[q, :, span(h)])

        @pl.when(is_end)
        def _():
            acc[q, :, span(h)] += extra[q, :, span(h)].astype(jnp.float32)

        if h is None:
            @pl.when(q % per_group == 0)
            def _():
                kv[...] = acc[q].astype(jnp.bfloat16)

            @pl.when(q % per_group > 0)
            def _():
                attend(q)

            retire(q)

            @pl.when(q >= 1)
            def _():
                retire_far(q - 1)

        else:
            attend(q, h)
            if h == 0:
                retire(q)
                retire_far(q - 1)

    each(last, far_step)
    far_step(last, 0)
    far_step(last, 1)

    lives = []
    for r in range(rollouts):
        live = lax.broadcasted_iota(jnp.int32, (slot, HEAD_SIZE), 0) < lengths[r]
        lives.append(jnp.sum(jnp.where(live, total[rows_of(r), :], jnp.float32(0.0)), axis=0, keepdims=True))
    partial = jnp.sum(jnp.concatenate(lives, axis=0), axis=1, keepdims=True)
    share_v[0] = jnp.broadcast_to(partial, share_v.shape[1:])
    for d in range(1, tp_count):
        start(always, base(("r", d), 1), share_v.at[0], tp_held.at[t], (g, t ^ d))
    tp_held[t] = share_v[0]
    for d in range(1, tp_count):
        arrived(always, base(("r", d), 1), tp_held.at[t ^ d])
    rewards = tp_held[0]
    for who in range(1, tp_count):
        rewards += tp_held[who]
    rewards = rewards / spans[...].astype(jnp.float32)
    lanes = lax.broadcasted_iota(jnp.int32, rewards.shape, 1)
    member = prompts[...] == lanes
    onehot = jnp.where(member, jnp.float32(1.0), jnp.float32(0.0))
    moments = [
        jnp.sum(v, axis=0, keepdims=True) for v in (onehot, onehot * rewards, onehot * (rewards * rewards))
    ]
    filler = jnp.zeros((rewards.shape[0] - 3, rewards.shape[1]), jnp.float32)
    share_v[1] = jnp.concatenate(moments + [filler], axis=0)
    grp_count = n * CORES
    for d in range(1, grp_count):
        start(always, base(("m", d), 1), share_v.at[1], grp_held.at[g], ((g + d) % grp_count, t))
    grp_held[g] = share_v[1]
    for d in range(1, grp_count):
        arrived(always, base(("m", d), 1), grp_held.at[(g + grp_count - d) % grp_count])
    summed = grp_held[0]
    for who in range(1, grp_count):
        summed += grp_held[who]
    divisor = jnp.maximum(summed[0:1], 1.0)
    average = summed[1:2] / divisor
    spread = summed[2:3] / divisor - average * average
    own_mean = jnp.sum(onehot * average, axis=1, keepdims=True)
    own_var = jnp.sum(onehot * spread, axis=1, keepdims=True)
    advantages[...] = (rewards - own_mean) / jnp.sqrt(own_var + 0.25)
    out_copy(last - 1).wait()
    for h in range(2):
        out_copy(last, h).wait()
        retire_far(last, h)
        sent(helper, local("p") + step_of(last, h), product(last, h))
    for d in range(1, tp_count):
        sent(always, base(("r", d), 1), share_v.at[0])
    for d in range(1, grp_count):
        sent(always, base(("m", d), 1), share_v.at[1])
    sent(is_end, base("t0", 1), token_rows(t))
    sent(is_end, base("t1", 1), token_rows(t))
    for d in range(1, twin):
        sent(helper, base(("g", d), 1), token_rows(t))


def fused(tokens, weight, lengths, prompt_of, score_weight, n, tp_count):
    rows, depth = tokens.shape
    own_rows = weight.shape[0]
    width = WIDTH
    chunks = weight.shape[1] // tp_count // width
    plane = own_rows * tp_count * CORES
    far = plane * (n - 2)
    steps, end_steps = n - 2, n // 2 - 1
    features = score_weight.shape[0]
    rollouts = lengths.shape[0]
    flows = (chunks + 1) * (tp_count + 1 + 3 * steps + end_steps) + 2 * tp_count + n * CORES
    slots = steps + end_steps
    anywhere = pl.BlockSpec(memory_space=pl.ANY)
    vmem = pl.BlockSpec(memory_space=pltpu.VMEM)
    attention, advantages, *_ = pl.pallas_call(
        functools.partial(fused_kernel, n, tp_count),
        in_specs=[pl.BlockSpec(memory_space=pltpu.SMEM), vmem, vmem, vmem, anywhere, anywhere],
        out_specs=[anywhere, vmem, anywhere, anywhere],
        out_shape=[
            jax.ShapeDtypeStruct((rows, features), jnp.bfloat16),
            jax.ShapeDtypeStruct((rollouts, HEAD_SIZE), jnp.float32),
            jax.ShapeDtypeStruct((chunks, depth, width), jnp.bfloat16),
            jax.ShapeDtypeStruct((rows, far), jnp.bfloat16),
        ],
        scratch_shapes=[
            pltpu.VMEM((rows, depth), jnp.bfloat16),
            pltpu.VMEM((rows, far), jnp.bfloat16),
            pltpu.VMEM((slots, plane, width), jnp.bfloat16),
            pltpu.VMEM((chunks, rows, width), jnp.float32),
            pltpu.VMEM((2, rows, width), jnp.bfloat16),
            pltpu.VMEM((chunks, rows, width), jnp.bfloat16),
            pltpu.VMEM((rows, 2 * HEAD_SIZE), jnp.bfloat16),
            pltpu.VMEM((2, rows, width), jnp.bfloat16),
            pltpu.VMEM((rows, HEAD_SIZE), jnp.float32),
            pltpu.VMEM((tp_count, rollouts, HEAD_SIZE), jnp.float32),
            pltpu.VMEM((n * CORES, rollouts, HEAD_SIZE), jnp.float32),
            pltpu.VMEM((2, rollouts, HEAD_SIZE), jnp.float32),
            pltpu.SemaphoreType.DMA((flows,)),
            pltpu.SemaphoreType.DMA((flows,)),
            pltpu.SemaphoreType.DMA((chunks,)),
            pltpu.SemaphoreType.DMA((slots,)),
            pltpu.SemaphoreType.DMA((3,)),
            pltpu.SemaphoreType.DMA((2,)),
        ],
        compiler_params=pltpu.CompilerParams(has_side_effects=True, vmem_limit_bytes=62 * 1024 * 1024),
    )(
        lengths, lengths.reshape(rollouts, 1), prompt_of,
        score_weight.reshape(features // width, width).astype(jnp.float32), tokens, weight,
    )
    return attention, advantages[:, 0]


def shards(tokens, joined_weight, rollout_lengths, prompt_of, score_weight):
    n = lax.axis_size("grp") // CORES
    tp_count = lax.axis_size("tp")
    return fused(tokens, joined_weight, rollout_lengths, prompt_of, score_weight, n, tp_count)


def solution(mesh):
    return jax.shard_map(
        shards,
        mesh=mesh,
        in_specs=(P("grp", None), P(("grp", "tp"), None), P("grp"), P("grp", None), P("tp")),
        out_specs=(P("grp", "tp"), P("grp")),
        check_vma=False,
    )
```

time: 307 us -> 284 us (0.925)
  Pallas kernels: 300 us -> 272 us
  local copies, waits for them, and re-layouts: 1.67 us -> 10 us
  other arithmetic: 3.25 us -> 0 us
    pallas_call x3 -> x1, Pallas kernels: 300 us -> 272 us  [fused(): pl.pallas_call(functools.partial(fused_kernel, n, tp_count), in_specs=[pl...]
    unnamed x6 -> x2, local copies, waits for them, and re-layouts: 0.02 us -> 6.11 us
where the time goes in v2:
time: 284 us; the launch traced here: 282 us
  Pallas kernels  272 us (96%)
  local copies, waits for them, and re-layouts  10 us (4%)
    pallas_call x1, Pallas kernels, fused(): pl.pallas_call(functools.partial(fused_kernel, n, tp_count), in_specs=[pl...  272 us
    unnamed x2, local copies, waits for them, and re-layouts  6.11 us

profile of v2, /device:TPU:0, one launch (start us, length us, event | category | flops | bytes accessed | tf_op | source)
XLA Modules:
  0.0 282.5 jit_solution(8698866538827864867)
XLA Ops:
  0.6 1.3 copy.10.prompts
  1.9 1.3 copy.9.spans
  3.3 1.3 reshape.11.score
  4.6 271.8 %shard_map.68 = (bf16[1024,2048]{1,0:T(8,128)(2,1)}, f32[8,128]{1,0:T(8,128)}, bf16[10,8192,256]{2,1,0:T(8,128)(2,1)}, bf16[1024,4096]{1,0:T(8,128)(2,1)}) custom-call(s32[8]{0:T(128)} %lengths.1, s32[8,1]{1,0:T(8,128)} %copy.9.spans, s32[8,1]{1,0:T(8,128)} %copy.10.prompts, f32[8,256]{1,0:T(8,128)} %reshape.11.score, bf16[1024,8192]{1,0:T(8,128)(2,1)} %tokens.1, ...), custom_call_target="tpu_custom_call" | custom-call | tf_op jit(solution)/shard_map/pallas_call | solution.py:492
  276.4 1.3 slice_reduce_fusion
  277.7 4.8 %copy.12 = bf16[1024,2048]{1,0:T(8,128)(2,1)} copy(bf16[1024,2048]{1,0:T(8,128)(2,1)} %get-tuple-element.8) | data formatting | bytes 8388608

commit v3 on v2

--- a/solution.py
+++ b/solution.py
@@ -16,7 +16,7 @@
 
 
 def fused_kernel(
-    n, tp_count, lengths, spans, prompts, score, tokens, weight, attention, advantages, gath, far,
+    n, tp_count, lengths, facts, tokens, weight, attention, advantages, gath, far,
     tok_v, far_v, w_v, acc, pbuf, extra, kv, mixed_v, total, tp_held, grp_held, share_v,
     send, recv, loads, w_sem, outs, misc,
 ):
@@ -111,11 +111,15 @@
         at = who * columns + (q // per_group * per_group + (q + per_group - 1) % per_group) * width
         return weight.at[:, pl.ds(pl.multiple_of(at, width), width)]
 
+    reached = {}
+    for s in range(1, n):
+        reached["end", s] = jnp.where(left, z - s >= 0, z + s <= n - 1)
+        reach = jnp.where(left, z + s <= n - 1, z - s >= 0)
+        reached["mid", s] = reach if s == 1 else reach & inner
+    passed = {s: reached["mid", s] & end_inner for s in range(1, n)}
+
     def has(side, s):
-        if side == "end":
-            return jnp.where(left, z - s >= 0, z + s <= n - 1)
-        reach = jnp.where(left, z + s <= n - 1, z - s >= 0)
-        return reach if s == 1 else reach & inner
+        return reached[side, s]
 
     def plane_of(side, s):
         return jnp.clip(z + sign * s if side == "mid" else z - sign * s, 0, n - 1)
@@ -149,7 +153,7 @@
         if side == "end":
             start(has(side, s), at, got, got, mid_device)
         else:
-            start(has(side, s) & end_inner, at, got, got, end_device)
+            start(passed[s], at, got, got, end_device)
 
     def handle(side, s, q, h=None):
         got = block(q, plane_of(side, s), core, h)
@@ -280,7 +284,7 @@
             for s in range(1, count + 1):
                 if s < steps:
                     there = has(side, s)
-                    sent(there if side == "end" else there & end_inner, flow(side, s + 1) + at, mine)
+                    sent(there if side == "end" else passed[s], flow(side, s + 1) + at, mine)
                 if s > 1:
                     sent(has(side, s), local((side, s)) + at, mine)
 
@@ -313,40 +317,51 @@
         elif h == 0:
             out_copy(q).wait()
         members = range(heads) if h is None else range(h * heads // 2, (h + 1) * heads // 2)
-        weights = score[pl.ds(index, 1), :]
-        for r in range(rollouts):
-            at = rows_of(r)
+        weights = [facts[pl.ds(index * heads + a, 1), :] for a in members]
+        count = len(members)
+        every = range(rollouts)
+        joined = [acc[q, rows_of(r), span(h)].astype(jnp.bfloat16) for r in every]
+        queries = [
+            jnp.concatenate([j[:, a * HEAD_SIZE : (a + 1) * HEAD_SIZE] for a in range(count)], axis=0)
+            for j in joined
+        ]
+        scores = [
+            lax.dot_general(
+                queries[r], kv[rows_of(r), :HEAD_SIZE], (((1,), (1,)), ((), ())),
+                preferred_element_type=jnp.float32,
+            )
+            for r in every
+        ]
+        mixed = []
+        for r in every:
             allowed = ((t_pos <= s_pos) & (t_pos < lengths[r]))[None]
-            joined = acc[q, at, span(h)].astype(jnp.bfloat16)
-            count = len(members)
-            queries = jnp.concatenate(
-                [joined[:, a * HEAD_SIZE : (a + 1) * HEAD_SIZE] for a in range(count)], axis=0
-            )
-            scores = lax.dot_general(
-                queries, kv[at, :HEAD_SIZE], (((1,), (1,)), ((), ())), preferred_element_type=jnp.float32
-            ) * HEAD_SIZE ** (-0.5)
-            scores = jnp.where(allowed, scores.reshape(count, slot, slot), jnp.float32(-1e30))
-            expo = jnp.exp(scores - jnp.max(scores, axis=-1, keepdims=True))
+            scaled = (scores[r] * HEAD_SIZE ** (-0.5)).reshape(count, slot, slot)
+            scaled = jnp.where(allowed, scaled, jnp.float32(-1e30))
+            expo = jnp.exp(scaled - jnp.max(scaled, axis=-1, keepdims=True))
             probs = expo * (1.0 / jnp.sum(expo, axis=-1, keepdims=True))
             probs = probs.astype(jnp.bfloat16).reshape(count * slot, slot)
-            mixed = jnp.dot(probs, kv[at, HEAD_SIZE:], preferred_element_type=jnp.float32).astype(jnp.bfloat16)
+            mixed.append(jnp.dot(probs, kv[rows_of(r), HEAD_SIZE:], preferred_element_type=jnp.float32))
+        for r in every:
+            at = rows_of(r)
+            rounded = mixed[r].astype(jnp.bfloat16)
             summed = total[at, :]
             for i, a in enumerate(members):
-                part_out = mixed[i * slot : (i + 1) * slot]
-                cols = slice(a * HEAD_SIZE, (a + 1) * HEAD_SIZE)
-                mixed_v[index % 2, at, cols] = part_out
-                summed += part_out.astype(jnp.float32) * weights[:, cols]
+                part_out = rounded[i * slot : (i + 1) * slot]
+                mixed_v[index % 2, at, slice(a * HEAD_SIZE, (a + 1) * HEAD_SIZE)] = part_out
+                summed += part_out.astype(jnp.float32) * weights[i]
             total[at, :] = summed
         out_copy(q, h).start()
 
     total[...] = jnp.zeros_like(total)
 
-    def far_step(q, h=None):
-        step = step_of(q, h)
+    def far_handles(q, h=None):
         for s in range(2, steps + 1):
             if s <= end_steps:
                 handle("end", s, q, h)
             handle("mid", s, q, h)
+
+    def far_step(q, h=None):
+        step = step_of(q, h)
         for side, s in others:
             if s > 1 or h != 1:
                 swapped(side, s, q, h if s > 1 else None)
@@ -355,42 +370,63 @@
             def _():
                 load(slot_of[side, s], q, plane_of(side, s), h).start()
 
+        def loaded(chosen):
+            for side, s in others:
+                if side == chosen:
+                    @pl.when(has(side, s))
+                    def _():
+                        load(slot_of[side, s], q, plane_of(side, s), h).wait()
+
+        loaded("mid")
+
+        @pl.when(helper)
+        def _():
+            if h != 1:
+                load(0, q, plane_of("mid", 1)).wait()
+
+            @pl.when(step >= 2)
+            def _():
+                sent(always, local("p") + step - 2, pbuf.at[step % 2])
+
+            for part_rows in (slice(0, rows // 2), slice(rows // 2, rows)):
+                whole = None
+                for s in range(1, steps + 1):
+                    cols = columns_at(plane_of("mid", s) - first_far)
+                    term = jnp.dot(
+                        far_v[part_rows, cols], w_v[slot_of["mid", s], :, span(h)],
+                        preferred_element_type=jnp.float32,
+                    )
+                    whole = term if whole is None else whole + term
+                pbuf[step % 2, part_rows, span(h)] = whole.astype(pbuf.dtype)
+                remote(
+                    local("p") + step, pbuf.at[step % 2, part_rows, span(h)],
+                    extra.at[q, part_rows, span(h)], end_device,
+                ).start()
+            if h is None:
+                load(0, q + 1, plane_of("mid", 1)).start()
+
+        if h is None:
+            @pl.when(q + 2 < chunks)
+            def _():
+                handle("end", 1, q + 2)
+
+        loaded("end")
         for side, s in others:
             @pl.when(has(side, s))
             def _():
-                load(slot_of[side, s], q, plane_of(side, s), h).wait()
-
-        @pl.when(helper)
-        def _():
-            if h != 1:
-                load(0, q, plane_of("mid", 1)).wait()
-
-            @pl.when(step >= 2)
-            def _():
-                sent(always, local("p") + step - 2, pbuf.at[step % 2])
-
-            whole = None
-            for s in range(1, steps + 1):
-                cols = columns_at(plane_of("mid", s) - first_far)
-                term = jnp.dot(
-                    far_v[:, cols], w_v[slot_of["mid", s], :, span(h)], preferred_element_type=jnp.float32
-                )
-                whole = term if whole is None else whole + term
-            pbuf[step % 2, :, span(h)] = whole.astype(pbuf.dtype)
-            remote(local("p") + step, product(q, h), extra.at[q, :, span(h)], end_device).start()
-            if h is None:
-                load(0, q + 1, plane_of("mid", 1)).start()
+                gemm(slot_of[side, s], q, plane_of(side, s), False, h)
 
         if h is None:
-            @pl.when(q + 2 < chunks)
-            def _():
-                handle("end", 1, q + 2)
-
-        for side, s in others:
-            @pl.when(has(side, s))
-            def _():
-                gemm(slot_of[side, s], q, plane_of(side, s), False, h)
-
+            @pl.when(q + 1 < last)
+            def _():
+                far_handles(q + 1)
+
+            @pl.when(q + 1 == last)
+            def _():
+                far_handles(last, 0)
+
+        elif h == 0:
+            far_handles(last, 1)
         arrived(is_end, local("p") + step, extra.at[q, :, span(h)])
 
         @pl.when(is_end)
@@ -418,6 +454,7 @@
                 retire(q)
                 retire_far(q - 1)
 
+    far_handles(0)
     each(last, far_step)
     far_step(last, 0)
     far_step(last, 1)
@@ -436,9 +473,10 @@
     rewards = tp_held[0]
     for who in range(1, tp_count):
         rewards += tp_held[who]
-    rewards = rewards / spans[...].astype(jnp.float32)
+    features = facts.shape[0] - 2 * rollouts
+    rewards = rewards / facts[features : features + rollouts]
     lanes = lax.broadcasted_iota(jnp.int32, rewards.shape, 1)
-    member = prompts[...] == lanes
+    member = facts[features + rollouts :] == lanes.astype(jnp.float32)
     onehot = jnp.where(member, jnp.float32(1.0), jnp.float32(0.0))
     moments = [
         jnp.sum(v, axis=0, keepdims=True) for v in (onehot, onehot * rewards, onehot * (rewards * rewards))
@@ -487,11 +525,18 @@
     rollouts = lengths.shape[0]
     flows = (chunks + 1) * (tp_count + 1 + 3 * steps + end_steps) + 2 * tp_count + n * CORES
     slots = steps + end_steps
+    small = jnp.concatenate([lengths, prompt_of[:, 0]]).astype(jnp.float32)
+    table = jnp.concatenate(
+        [
+            score_weight.reshape(features // HEAD_SIZE, HEAD_SIZE).astype(jnp.float32),
+            jnp.broadcast_to(small[:, None], (2 * rollouts, HEAD_SIZE)),
+        ]
+    )
     anywhere = pl.BlockSpec(memory_space=pl.ANY)
     vmem = pl.BlockSpec(memory_space=pltpu.VMEM)
     attention, advantages, *_ = pl.pallas_call(
         functools.partial(fused_kernel, n, tp_count),
-        in_specs=[pl.BlockSpec(memory_space=pltpu.SMEM), vmem, vmem, vmem, anywhere, anywhere],
+        in_specs=[pl.BlockSpec(memory_space=pltpu.SMEM), vmem, anywhere, anywhere],
         out_specs=[anywhere, vmem, anywhere, anywhere],
         out_shape=[
             jax.ShapeDtypeStruct((rows, features), jnp.bfloat16),
@@ -520,10 +565,7 @@
             pltpu.SemaphoreType.DMA((2,)),
         ],
         compiler_params=pltpu.CompilerParams(has_side_effects=True, vmem_limit_bytes=62 * 1024 * 1024),
-    )(
-        lengths, lengths.reshape(rollouts, 1), prompt_of,
-        score_weight.reshape(features // width, width).astype(jnp.float32), tokens, weight,
-    )
+    )(lengths, table, tokens, weight)
     return attention, advantages[:, 0]
 
 

time: 284 us -> 280 us (0.986)
  local copies, waits for them, and re-layouts: 10 us -> 6.17 us
    unnamed x2 -> x1, local copies, waits for them, and re-layouts: 6.11 us -> 4.79 us
where the time goes in v3:
time: 280 us; the launch traced here: 279 us
  Pallas kernels  270 us (96%)
  local copies, waits for them, and re-layouts  6.17 us (2%)
    pallas_call x1, Pallas kernels, fused(): pl.pallas_call(functools.partial(fused_kernel, n, tp_count), in_specs=[pl...  270 us

profile of v3, /device:TPU:0, one launch (start us, length us, event | category | flops | bytes accessed | tf_op | source)
XLA Modules:
  0.0 278.9 jit_solution(1976289380638663305)
XLA Ops:
  0.6 0.7 add_convert_fusion
  1.4 0.1 pad.1.clone
  1.5 0.7 bitcast_convert_fusion
  2.1 0.7 pad_maximum_fusion.facts
  2.8 270.0 %shard_map.68 = (bf16[1024,2048]{1,0:T(8,128)(2,1)}, f32[8,128]{1,0:T(8,128)}, bf16[10,8192,256]{2,1,0:T(8,128)(2,1)}, bf16[1024,4096]{1,0:T(8,128)(2,1)}) custom-call(s32[8]{0:T(128)} %lengths.1, f32[32,128]{1,0:T(8,128)} %pad_maximum_fusion.facts, bf16[1024,8192]{1,0:T(8,128)(2,1)} %tokens.1, bf16[256,10240]{1,0:T(8,128)(2,1)} %weight.1), custom_call_target="tpu_custom_call" | custom-call | tf_op jit(solution)/shard_map/pallas_call | solution.py:537
  272.8 1.3 slice_reduce_fusion
  274.1 4.8 %copy.8 = bf16[1024,2048]{1,0:T(8,128)(2,1)} copy(bf16[1024,2048]{1,0:T(8,128)(2,1)} %get-tuple-element.8) | data formatting | bytes 8388608
